TPU v7x, 32 devices: a whole 2x2x4 slice. The times are simulated.
32 devices in a mesh: tensor: 8 (over z, x), expert: 2 (over core), dp: 2 (over y).
Axes of the slice: x: 2, y: 2, z: 4, core: 2. Of those that a mesh axis runs over, the one named last changes fastest.
Arguments:
- tokens: bfloat16 [512, 2048], P(('expert', 'dp')), may hold values from -6 to 6
- tangent: bfloat16 [512, 2048], P(('expert', 'dp')), may hold values from -6 to 6
- cotangent: bfloat16 [512, 2048], P(('expert', 'dp')), may hold values from -0.59765625 to 0.59765625
- expert_ids: int32 [512, 8], P(('expert', 'dp')), may hold values from 0 to 15, all different within a row; in each aligned block of 128 rows (0 to 127, 128 to 255, ...) at most 96 rows name the same one
- gates: float32 [512, 8], P(('expert', 'dp')), may hold values from 0.1 to 1
- w_in: bfloat16 [16, 2, 768, 2048], P(('tensor', 'expert'), None, None, 'dp'), may hold values from -0.125 to 0.125
- v_in: bfloat16 [16, 2, 768, 2048], P(('tensor', 'expert'), None, None, 'dp'), may hold values from -0.125 to 0.125
- w_out: bfloat16 [16, 768, 2048], P(('tensor', 'expert'), None, 'dp'), may hold values from -0.21875 to 0.21875
- v_out: bfloat16 [16, 768, 2048], P(('tensor', 'expert'), None, 'dp'), may hold values from -0.21875 to 0.21875
Outputs:
- hvp_tokens: float32 [512, 2048], P(('expert', 'dp'))
- hvp_in: float32 [16, 2, 768, 2048], P(('tensor', 'expert'), None, None, 'dp')
- hvp_out: float32 [16, 768, 2048], P(('tensor', 'expert'), None, 'dp')
Inputs may be any that keep to these rules, and one draw needn't show every extreme that they name: `expert_ids`: each token names 8 different experts; among the tokens of one block of 128 no expert is named more than 96 times, and some expert reaches 96 in some blocks.
All inputs are finite; a program needn't handle non-finite values.
Results may differ from a plain program's by a relative error of at most 0.013.
Values may be sent and summed in bfloat16 or wider, within the bound.
A program may use at most 128 MiB of HBM per device.

v0:
```python
import jax
import jax.numpy as jnp
from jax import lax
from jax.sharding import PartitionSpec as P


def expert_terms(rows_x, rows_u, rows_dy, w_in, v_in, w_out, v_out):
    f32 = jnp.float32
    pre = jnp.einsum("nesd,egfd->nesgf", rows_x, w_in, preferred_element_type=f32)
    pre_dot = jnp.einsum("nesd,egfd->nesgf", rows_u, w_in, preferred_element_type=f32)
    pre_dot = pre_dot + jnp.einsum("nesd,egfd->nesgf", rows_x, v_in, preferred_element_type=f32)
    gate_pre, up_val = (pre[:, :, :, 0], pre[:, :, :, 1])
    gate_dot, up_dot = (pre_dot[:, :, :, 0], pre_dot[:, :, :, 1])
    back = jnp.einsum("nesd,efd->nesf", rows_dy, w_out, preferred_element_type=f32)
    back_dot = jnp.einsum("nesd,efd->nesf", rows_dy, v_out, preferred_element_type=f32)
    sigma = jax.nn.sigmoid(gate_pre)
    silu_val = gate_pre * sigma
    first = sigma * (1.0 + gate_pre * (1.0 - sigma))
    second = sigma * (1.0 - sigma) * (2.0 + gate_pre * (1.0 - 2.0 * sigma))
    grad_a = back * up_val * first
    grad_b = back * silu_val
    tang_a = back_dot * up_val * first + back * up_dot * first + back * up_val * second * gate_dot
    tang_b = back_dot * silu_val + back * first * gate_dot
    grads = jnp.stack([grad_a, grad_b], axis=3).astype(jnp.bfloat16)
    tangs = jnp.stack([tang_a, tang_b], axis=3).astype(jnp.bfloat16)
    hidden_dot = (first * gate_dot * up_val + silu_val * up_dot).astype(jnp.bfloat16)
    partial_value = jnp.einsum("nesgf,egfd->nesd", tangs, w_in, preferred_element_type=f32)
    partial_value = partial_value + jnp.einsum(
        "nesgf,egfd->nesd", grads, v_in, preferred_element_type=f32
    )
    part_in = jnp.einsum("nesd,nesgf->egfd", rows_u, grads, preferred_element_type=f32)
    part_in = part_in + jnp.einsum("nesd,nesgf->egfd", rows_x, tangs, preferred_element_type=f32)
    part_out = jnp.einsum("nesf,nesd->efd", hidden_dot, rows_dy, preferred_element_type=f32)
    return (partial_value.astype(jnp.bfloat16), part_in, part_out)


def shards(tokens, tangent, cotangent, expert_ids, gates, w_in, v_in, w_out, v_out):
    n_tensor = lax.axis_size("tensor")
    n_expert = lax.axis_size("expert")
    rank = lax.axis_index("tensor")
    local_experts = w_in.shape[0]
    all_experts = local_experts * n_tensor * n_expert
    tok_rows, width = tokens.shape
    topk = expert_ids.shape[1]
    share = min(tok_rows // n_tensor, 3 * tok_rows * topk // (2 * all_experts * n_tensor))
    full_in, full_v_in, full_out, full_v_out = (
        lax.all_gather(w_in, "dp", axis=3, tiled=True),
        lax.all_gather(v_in, "dp", axis=3, tiled=True),
        lax.all_gather(w_out, "dp", axis=2, tiled=True),
        lax.all_gather(v_out, "dp", axis=2, tiled=True),
    )
    picks = expert_ids.reshape(-1)
    onehot = (picks[:, None] == jnp.arange(all_experts, dtype=jnp.int32)[None, :]).astype(jnp.int32)
    running = jnp.cumsum(onehot, axis=0) - 1
    slots = jnp.sum(onehot * running, axis=1)
    owned = slots // share == rank
    limit = all_experts * share
    target = jnp.where(owned, picks * share + slots % share, limit)
    scale = gates.reshape(-1)
    rows_x = jnp.repeat(tokens, topk, axis=0)
    rows_u = jnp.repeat(tangent, topk, axis=0)
    rows_dy = (scale[:, None] * jnp.repeat(cotangent, topk, axis=0).astype(jnp.float32)).astype(
        jnp.bfloat16
    )
    empty = jnp.zeros((limit, width), jnp.bfloat16)
    wide_shape = (n_tensor * n_expert, local_experts, share, width)
    send_x = empty.at[target].set(rows_x, mode="drop").reshape(wide_shape)
    send_u = empty.at[target].set(rows_u, mode="drop").reshape(wide_shape)
    send_dy = empty.at[target].set(rows_dy, mode="drop").reshape(wide_shape)
    got_x, got_u, got_dy = (
        lax.all_to_all(send_x, ("tensor", "expert"), split_axis=0, concat_axis=0, tiled=True),
        lax.all_to_all(send_u, ("tensor", "expert"), split_axis=0, concat_axis=0, tiled=True),
        lax.all_to_all(send_dy, ("tensor", "expert"), split_axis=0, concat_axis=0, tiled=True),
    )
    partial_value, part_in, part_out = expert_terms(
        got_x, got_u, got_dy, full_in, full_v_in, full_out, full_v_out
    )
    returned = lax.all_to_all(
        partial_value, ("tensor", "expert"), split_axis=0, concat_axis=0, tiled=True
    )
    table = returned.astype(jnp.float32).reshape(limit, width)
    picked = table[jnp.minimum(target, limit - 1)]
    picked = jnp.where(owned[:, None], picked, 0.0)
    own_sums = jnp.sum(picked.reshape(tok_rows, topk, width), axis=1)
    hvp_tokens = lax.psum(own_sums.astype(jnp.bfloat16), "tensor").astype(jnp.float32)
    hvp_in, hvp_out = (
        lax.psum_scatter(
            part_in.astype(jnp.bfloat16), "dp", scatter_dimension=3, tiled=True
        ).astype(jnp.float32),
        lax.psum_scatter(
            part_out.astype(jnp.bfloat16), "dp", scatter_dimension=2, tiled=True
        ).astype(jnp.float32),
    )
    return (hvp_tokens, hvp_in, hvp_out)


def solution(mesh):
    placed = (
        P(("expert", "dp"), None),
        P(("expert", "dp"), None),
        P(("expert", "dp"), None),
        P(("expert", "dp"), None),
        P(("expert", "dp"), None),
        P(("tensor", "expert"), None, None, "dp"),
        P(("tensor", "expert"), None, None, "dp"),
        P(("tensor", "expert"), None, "dp"),
        P(("tensor", "expert"), None, "dp"),
    )
    return jax.shard_map(
        shards,
        mesh=mesh,
        in_specs=placed,
        out_specs=(
            P(("expert", "dp"), None),
            P(("tensor", "expert"), None, None, "dp"),
            P(("tensor", "expert"), None, "dp"),
        ),
        check_vma=False,
    )
```

profile of v0, /device:TPU:0, one launch (start us, length us, event | category | flops | bytes accessed | tf_op | source)
XLA Modules:
  0.0 534.4 jit_solution(1958558635749751632)
XLA Ops:
  15.0 6.5 %scatter_custom_fusion.1 = bf16[192,2048]{1,0:T(8,128)(2,1)S(1)} fusion(s32[1024]{0:T(1024)S(1)} %bitcast.255, bf16[128,2048]{1,0:T(8,128)(2,1)S(1)} %copy-done, bf16[]{:T(256)} %constant.42.clone.1), kind=kCustom, calls=%fused_computation.25 | custom fusion | bytes 1310722 | tf_op jit(solution)/shard_map/scatter | solution.py:67
  22.7 7.4 %all-to-all-start.1 = ((bf16[16,1,12,2048]{3,2,1,0:T(8,128)(2,1)}), bf16[16,1,12,2048]{3,2,1,0:T(8,128)(2,1)S(1)}, u32[]{:S(2)}, u32[]{:S(2)}) async-start(bf16[16,1,12,2048]{3,2,1,0:T(8,128)(2,1)} %bitcast.14), calls=%async_computation.1 | async-start | bytes 2097152 | tf_op jit(solution)/shard_map/all_to_all | solution.py:71
  30.5 6.9 %scatter_custom_fusion = bf16[192,2048]{1,0:T(8,128)(2,1)S(1)} fusion(s32[1024]{0:T(1024)S(1)} %bitcast.256, f32[128,2048]{1,0:T(8,128)S(1)} %convert_element_type.72, f32[1024]{0:T(1024)S(1)} %mul.184, bf16[]{:T(256)} %constant.42.clone.1), kind=kCustom, calls=%fused_computation.22 | custom fusion | flops 4194304 | bytes 1839106 | tf_op jit(solution)/shard_map/scatter | solution.py:69
  38.6 14.5 %all-to-all-done.1 = bf16[16,1,12,2048]{3,2,1,0:T(8,128)(2,1)S(1)} async-done(((bf16[16,1,12,2048]{3,2,1,0:T(8,128)(2,1)}), bf16[16,1,12,2048]{3,2,1,0:T(8,128)(2,1)S(1)}, u32[]{:S(2)}, u32[]{:S(2)}) %all-to-all-start.1) | async-done | bytes 786464 | tf_op jit(solution)/shard_map/all_to_all | solution.py:71
  53.0 6.8 %all-to-all-start = ((bf16[16,1,12,2048]{3,2,1,0:T(8,128)(2,1)}), bf16[16,1,12,2048]{3,2,1,0:T(8,128)(2,1)S(1)}, u32[]{:S(2)}, u32[]{:S(2)}) async-start(bf16[16,1,12,2048]{3,2,1,0:T(8,128)(2,1)} %bitcast.6), calls=%async_computation | async-start | bytes 2097152 | tf_op jit(solution)/shard_map/all_to_all | solution.py:73
  60.4 6.5 %scatter_custom_fusion.2 = bf16[192,2048]{1,0:T(8,128)(2,1)S(1)} fusion(s32[1024]{0:T(1024)S(1)} %bitcast.257, bf16[128,2048]{1,0:T(8,128)(2,1)S(1)} %copy-done.9, bf16[]{:T(256)} %constant.42.clone.1), kind=kCustom, calls=%fused_computation.23 | custom fusion | bytes 1310722 | tf_op jit(solution)/shard_map/scatter | solution.py:68
  68.1 14.6 %all-to-all-done = bf16[16,1,12,2048]{3,2,1,0:T(8,128)(2,1)S(1)} async-done(((bf16[16,1,12,2048]{3,2,1,0:T(8,128)(2,1)}), bf16[16,1,12,2048]{3,2,1,0:T(8,128)(2,1)S(1)}, u32[]{:S(2)}, u32[]{:S(2)}) %all-to-all-start) | async-done | bytes 786464 | tf_op jit(solution)/shard_map/all_to_all | solution.py:73
  82.7 6.8 %all-to-all-start.2 = ((bf16[16,1,12,2048]{3,2,1,0:T(8,128)(2,1)}), bf16[16,1,12,2048]{3,2,1,0:T(8,128)(2,1)S(1)}, u32[]{:S(2)}, u32[]{:S(2)}) async-start(bf16[16,1,12,2048]{3,2,1,0:T(8,128)(2,1)} %bitcast.30), calls=%async_computation.2 | async-start | bytes 2097152 | tf_op jit(solution)/shard_map/all_to_all | solution.py:72
  92.9 46.3 %all-gather.7.cloned.1.call-done = bf16[1,2,768,2048]{3,2,1,0:T(8,128)(2,1)} async-done(((bf16[1,2,768,1024]{3,2,1,0:T(8,128)(2,1)}), bf16[1,2,768,2048]{3,2,1,0:T(8,128)(2,1)}) %all-gather.7.cloned.1.call-update) | async-done | bytes 6291472 | tf_op jit(solution)/shard_map/all_gather | solution.py:47
  139.1 6.4 %fusion.44 = f32[16,1,12,2,768]{4,0,2,3,1:T(8,128)} fusion(bf16[1,2,768,2048]{3,2,1,0:T(8,128)(2,1)} %all-gather.7.cloned.1.call-done, bf16[16,1,12,2048]{3,2,1,0:T(8,128)(2,1)} %copy-done.6), kind=kOutput, calls=%fused_computation.41 | convolution fusion | flops 1207959552 | bytes 8257536 | tf_op jit(solution)/shard_map/nesd,egfd->nesgf/dot_general | solution.py:9
  145.6 75.5 %all-gather.11.cloned.1.call-done = bf16[1,2,768,2048]{3,2,1,0:T(8,128)(2,1)} async-done(((bf16[1,2,768,1024]{3,2,1,0:T(8,128)(2,1)}), bf16[1,2,768,2048]{3,2,1,0:T(8,128)(2,1)}) %all-gather.11.cloned.1.call-update) | async-done | bytes 6291472 | tf_op jit(solution)/shard_map/all_gather | solution.py:48
  221.1 6.4 %fusion.6 = f32[16,12,2,768]{3,0,1,2:T(8,128)} fusion(bf16[1,2,768,2048]{3,2,1,0:T(8,128)(2,1)} %all-gather.11.cloned.1.call-done, bf16[16,1,12,2048]{3,2,1,0:T(8,128)(2,1)} %copy-done.6), kind=kOutput, calls=%fused_computation.14 | convolution fusion | flops 1207959552 | bytes 8257536 | tf_op jit(solution)/shard_map/nesd,egfd->nesgf/dot_general | solution.py:11
  227.5 7.6 %fusion.50 = f32[16,1,12,2,768]{4,0,2,3,1:T(8,128)} fusion(f32[16,12,2,768]{3,0,1,2:T(8,128)} %fusion.6, bf16[1,2,768,2048]{3,2,1,0:T(8,128)(2,1)} %all-gather.7.cloned.1.call-done, bf16[16,1,12,2048]{3,2,1,0:T(8,128)(2,1)S(1)} %all-to-all-done.2), kind=kOutput, calls=%fused_computation.43 | convolution fusion | flops 1208254464 | bytes 9437184 | tf_op jit(solution)/shard_map/nesd,egfd->nesgf/dot_general | solution.py:10
  235.1 32.3 %all-gather.9.cloned.1.call-done = bf16[1,768,2048]{2,1,0:T(8,128)(2,1)} async-done(((bf16[1,768,1024]{2,1,0:T(8,128)(2,1)}), bf16[1,768,2048]{2,1,0:T(8,128)(2,1)}) %all-gather.9.cloned.1.call-update) | async-done | bytes 3145744 | tf_op jit(solution)/shard_map/all_gather | solution.py:49
  279.5 5.6 %all-to-all-start.3 = ((bf16[16,1,12,2048]{3,2,1,0:T(8,128)(2,1)}), bf16[16,1,12,2048]{3,2,1,0:T(8,128)(2,1)S(1)}, u32[]{:S(2)}, u32[]{:S(2)}) async-start(bf16[16,1,12,2048]{3,2,1,0:T(8,128)(2,1)} %copy.48), calls=%async_computation.3 | async-start | bytes 2097152 | tf_op jit(solution)/shard_map/all_to_all | solution.py:78
  285.6 22.4 %all-to-all-done.3 = bf16[16,1,12,2048]{3,2,1,0:T(8,128)(2,1)S(1)} async-done(((bf16[16,1,12,2048]{3,2,1,0:T(8,128)(2,1)}), bf16[16,1,12,2048]{3,2,1,0:T(8,128)(2,1)S(1)}, u32[]{:S(2)}, u32[]{:S(2)}) %all-to-all-start.3) | async-done | bytes 786464 | tf_op jit(solution)/shard_map/all_to_all | solution.py:78
  308.2 6.9 %gather_fusion = f32[1024,2048]{1,0:T(8,128)} fusion(f32[192,2048]{1,0:T(8,128)S(1)} %reshape.392, s32[1024]{0:T(1024)S(1)} %broadcast_clamp_fusion), kind=kCustom, calls=%fused_computation | custom fusion | bytes 16781312 | tf_op jit(solution)/shard_map/gather | solution.py:82
  315.1 7.7 %fusion.1 = bf16[128,2048]{1,0:T(8,128)(2,1)} fusion(f32[1024,2048]{1,0:T(8,128)} %gather_fusion, pred[128,8]{1,0:T(8,128)(4,1)S(1)} %fusion.99), kind=kLoop, calls=%fused_computation.7 | loop fusion | flops 3932160 | bytes 8913920 | tf_op jit(solution)/shard_map/reduce_sum | solution.py:84
  322.9 4.7 fusion.26
  329.7 4.8 fusion.3
  334.6 62.3 %all-reduce.2.cloned.1.call-done = bf16[128,2048]{1,0:T(8,128)(2,1)} async-done(((bf16[128,2048]{1,0:T(8,128)(2,1)}), bf16[128,2048]{1,0:T(8,128)(2,1)}) %all-reduce.2.cloned.1.call-update) | async-done | bytes 524304 | tf_op jit(solution)/shard_map/psum | solution.py:85
  399.0 43.2 %reduce-scatter.5.cloned.1.call-done = bf16[1,768,1024]{2,1,0:T(8,128)(2,1)} async-done(((bf16[1,768,2048]{2,1,0:T(8,128)(2,1)}), bf16[1,768,1024]{2,1,0:T(8,128)(2,1)}) %reduce-scatter.5.cloned.1.call-update) | async-done | bytes 1572880 | tf_op jit(solution)/shard_map/reduce_scatter | solution.py:90
  445.7 76.5 %reduce-scatter.3.cloned.1.call-done = bf16[1,2,768,1024]{3,2,1,0:T(8,128)(2,1)} async-done(((bf16[1,2,768,2048]{3,2,1,0:T(8,128)(2,1)}), bf16[1,2,768,1024]{3,2,1,0:T(8,128)(2,1)}) %reduce-scatter.3.cloned.1.call-update) | async-done | bytes 3145744 | tf_op jit(solution)/shard_map/reduce_scatter | solution.py:87
  522.2 5.3 convert_element_type.83
  (95 shorter events, 35.7 us)
Async XLA Ops:
  7.2 7.9 %copy-start = (bf16[128,2048]{1,0:T(8,128)(2,1)S(1)}, bf16[128,2048]{1,0:T(8,128)(2,1)}, u32[]{:S(2)}) copy-start(bf16[128,2048]{1,0:T(8,128)(2,1)} %param.9) | copy-start | bytes 1572868
  7.2 82.3 %all-gather.5.cloned.1.call-start = ((), (), s32[]{:S(2)}) async-start(), calls=%async_computation.6 | async-start | bytes 4718592 | tf_op jit(solution)/shard_map/all_gather | solution.py:50
  7.9 131.2 %all-gather.7.cloned.1.call-start = ((), (), s32[]{:S(2)}) async-start(), calls=%async_computation.7 | async-start | bytes 9437184 | tf_op jit(solution)/shard_map/all_gather | solution.py:47
  8.7 21.4 %copy-start.11 = (f32[128,8]{0,1:T(8,128)S(1)}, f32[128,8]{0,1:T(8,128)}, u32[]{:S(2)}) copy-start(f32[128,8]{0,1:T(8,128)} %param.13) | copy-start | bytes 12292
  8.7 21.6 %copy-start.8 = (bf16[128,2048]{1,0:T(8,128)(2,1)S(1)}, bf16[128,2048]{1,0:T(8,128)(2,1)}, u32[]{:S(2)}) copy-start(bf16[128,2048]{1,0:T(8,128)(2,1)} %param.11) | copy-start | bytes 1572868
  8.7 212.4 %all-gather.11.cloned.1.call-start = ((), (), s32[]{:S(2)}) async-start(), calls=%async_computation.9 | async-start | bytes 9437184 | tf_op jit(solution)/shard_map/all_gather | solution.py:48
  22.7 30.3 %all-to-all-start.1 = ((bf16[16,1,12,2048]{3,2,1,0:T(8,128)(2,1)}), bf16[16,1,12,2048]{3,2,1,0:T(8,128)(2,1)S(1)}, u32[]{:S(2)}, u32[]{:S(2)}) async-start(bf16[16,1,12,2048]{3,2,1,0:T(8,128)(2,1)} %bitcast.14), calls=%async_computation.1 | async-start | bytes 2097152 | tf_op jit(solution)/shard_map/all_to_all | solution.py:71
  30.3 30.1 %copy-start.9 = (bf16[128,2048]{1,0:T(8,128)(2,1)S(1)}, bf16[128,2048]{1,0:T(8,128)(2,1)}, u32[]{:S(2)}) copy-start(bf16[128,2048]{1,0:T(8,128)(2,1)} %param.10) | copy-start | bytes 1572868
  53.0 29.7 %copy-start.6 = (bf16[16,1,12,2048]{3,2,1,0:T(8,128)(2,1)}, bf16[16,1,12,2048]{3,2,1,0:T(8,128)(2,1)S(1)}, u32[]{:S(2)}) copy-start(bf16[16,1,12,2048]{3,2,1,0:T(8,128)(2,1)S(1)} %all-to-all-done.1) | copy-start | bytes 2359300
  53.0 29.7 %all-to-all-start = ((bf16[16,1,12,2048]{3,2,1,0:T(8,128)(2,1)}), bf16[16,1,12,2048]{3,2,1,0:T(8,128)(2,1)S(1)}, u32[]{:S(2)}, u32[]{:S(2)}) async-start(bf16[16,1,12,2048]{3,2,1,0:T(8,128)(2,1)} %bitcast.6), calls=%async_computation | async-start | bytes 2097152 | tf_op jit(solution)/shard_map/all_to_all | solution.py:73
  59.8 207.6 %all-gather.9.cloned.1.call-start = ((), (), s32[]{:S(2)}) async-start(), calls=%async_computation.8 | async-start | bytes 4718592 | tf_op jit(solution)/shard_map/all_gather | solution.py:49
  82.7 184.7 %copy-start.4 = (bf16[16,1,12,2048]{3,2,1,0:T(8,128)(2,1)}, bf16[16,1,12,2048]{3,2,1,0:T(8,128)(2,1)S(1)}, u32[]{:S(2)}) copy-start(bf16[16,1,12,2048]{3,2,1,0:T(8,128)(2,1)S(1)} %all-to-all-done) | copy-start | bytes 2359300
  82.7 144.8 %all-to-all-start.2 = ((bf16[16,1,12,2048]{3,2,1,0:T(8,128)(2,1)}), bf16[16,1,12,2048]{3,2,1,0:T(8,128)(2,1)S(1)}, u32[]{:S(2)}, u32[]{:S(2)}) async-start(bf16[16,1,12,2048]{3,2,1,0:T(8,128)(2,1)} %bitcast.30), calls=%async_computation.2 | async-start | bytes 2097152 | tf_op jit(solution)/shard_map/all_to_all | solution.py:72
  227.5 7.6 %copy-start.2 = (bf16[16,1,12,2048]{3,2,1,0:T(8,128)(2,1)}, bf16[16,1,12,2048]{3,2,1,0:T(8,128)(2,1)S(1)}, u32[]{:S(2)}) copy-start(bf16[16,1,12,2048]{3,2,1,0:T(8,128)(2,1)S(1)} %all-to-all-done.2) | copy-start | bytes 2359300
  267.4 9.1 %slice-start = ((s8[6291456]{0:T(1024)(128)(4,1)}), s8[2097152]{0:T(1024)(128)(4,1)S(1)}, s32[]{:S(2)}) async-start(s8[6291456]{0:T(1024)(128)(4,1)} %bitcast.258), calls=%async_computation.13 | async-start | bytes 4194304
  272.0 4.6 slice-start.1
  279.5 28.5 %all-to-all-start.3 = ((bf16[16,1,12,2048]{3,2,1,0:T(8,128)(2,1)}), bf16[16,1,12,2048]{3,2,1,0:T(8,128)(2,1)S(1)}, u32[]{:S(2)}, u32[]{:S(2)}) async-start(bf16[16,1,12,2048]{3,2,1,0:T(8,128)(2,1)} %copy.48), calls=%async_computation.3 | async-start | bytes 2097152 | tf_op jit(solution)/shard_map/all_to_all | solution.py:78
  285.1 111.7 %all-reduce.2.cloned.1.call-start = ((), (), s32[]{:S(2)}) async-start(), calls=%async_computation.10 | async-start | bytes 1048576 | tf_op jit(solution)/shard_map/psum | solution.py:85
  315.1 7.8 %copy-start.5 = (bf16[16,1,12,2048]{3,2,1,0:T(8,128)(2,1)S(1)}, bf16[16,1,12,2048]{3,2,1,0:T(8,128)(2,1)}, u32[]{:S(2)}) copy-start(bf16[16,1,12,2048]{3,2,1,0:T(8,128)(2,1)} %copy-done.4) | copy-start | bytes 2359300
  322.8 4.9 copy-start.3
  322.8 4.9 copy-start.13
  322.8 119.3 %reduce-scatter.5.cloned.1.call-start = ((), (), s32[]{:S(2)}) async-start(), calls=%async_computation.12 | async-start | bytes 4718592 | tf_op jit(solution)/shard_map/reduce_scatter | solution.py:90
  327.7 194.5 %reduce-scatter.3.cloned.1.call-start = ((), (), s32[]{:S(2)}) async-start(), calls=%async_computation.11 | async-start | bytes 9437184 | tf_op jit(solution)/shard_map/reduce_scatter | solution.py:87
  442.2 85.4 %copy-start.1 = (bf16[128,2048]{1,0:T(8,128)(2,1)S(1)}, bf16[128,2048]{1,0:T(8,128)(2,1)}, u32[]{:S(2)}) copy-start(bf16[128,2048]{1,0:T(8,128)(2,1)} %param.9) | copy-start | bytes 1572868
  (7 other events, 22.1 us)
Sparse Core Ops, SparseCore 0:
  9.5 47.6 all-gather.4
  58.8 80.3 all-gather.6
  140.7 80.3 all-gather.10
  222.5 44.8 all-gather.8
  322.9 73.8 all-reduce.1
  399.5 42.6 reduce-scatter.4
  445.1 77.1 reduce-scatter.2
where the time goes:
time: 535 us; the launch traced here: 534 us
  waiting for transfers between devices  390 us (73%)
  matrix products  45.7 us (9%)
  other arithmetic  30.5 us (6%)
  starting transfers between devices  27.3 us (5%)
  local copies, waits for them, and re-layouts  26.2 us (5%)
  between operations  14.6 us (3%)
    reduce_scatter x1, waiting for transfers between devices, shards(): lax.psum_scatter(part_in.astype(jnp.bfloat16), 'dp', scatter_dimension=3,...  76.5 us
    all_gather x1, waiting for transfers between devices, shards(): lax.all_gather(v_in, 'dp', axis=3, tiled=True)  75.5 us
    psum x1, waiting for transfers between devices, shards(): lax.psum(own_sums.astype(jnp.bfloat16), 'tensor').astype(jnp.float32)  62.3 us
    all_gather x1, waiting for transfers between devices, shards(): lax.all_gather(w_in, 'dp', axis=3, tiled=True)  46.3 us
    reduce_scatter x1, waiting for transfers between devices, shards(): lax.psum_scatter(part_out.astype(jnp.bfloat16), 'dp', scatter_dimension=2...  43.2 us
    all_gather x1, waiting for transfers between devices, shards(): lax.all_gather(w_out, 'dp', axis=2, tiled=True)  32.3 us
    all_to_all x1, waiting for transfers between devices, shards(): lax.all_to_all(partial_value, ('tensor', 'expert'), split_axis=0, concat_...  22.4 us
    all_to_all x1, waiting for transfers between devices, shards(): lax.all_to_all(send_dy, ('tensor', 'expert'), split_axis=0, concat_axis=0...  14.6 us
  transfers between devices with their start and end apart: 11, of which 9 were waited for; matrix products, arithmetic and copies ran while one was open for 13% of the time, Pallas kernels for 0%

commit v1 on v0

--- a/solution.py
+++ b/solution.py
@@ -82,7 +82,9 @@
     picked = table[jnp.minimum(target, limit - 1)]
     picked = jnp.where(owned[:, None], picked, 0.0)
     own_sums = jnp.sum(picked.reshape(tok_rows, topk, width), axis=1)
-    hvp_tokens = lax.psum(own_sums.astype(jnp.bfloat16), "tensor").astype(jnp.float32)
+    hvp_tokens = jnp.sum(lax.all_gather(own_sums.astype(jnp.bfloat16), "tensor"), axis=0).astype(
+        jnp.float32
+    )
     hvp_in, hvp_out = (
         lax.psum_scatter(
             part_in.astype(jnp.bfloat16), "dp", scatter_dimension=3, tiled=True

time: 535 us -> 489 us (0.914)
  waiting for transfers between devices: 390 us -> 345 us
    all_gather x0 -> x1, waiting for transfers between devices: none -> 62.4 us  [shards(): lax.all_gather(own_sums.astype(jnp.bfloat16), 'tensor')]
    psum x1 -> x0, waiting for transfers between devices: 62.3 us -> none  [shards(): lax.psum(own_sums.astype(jnp.bfloat16), 'tensor').astype(jnp.float32)]
    all_gather x1, waiting for transfers between devices: 46.3 us -> 2.89 us  [shards(): lax.all_gather(w_in, 'dp', axis=3, tiled=True)]
    reduce_scatter x1, waiting for transfers between devices: 43.2 us -> 0.02 us  [shards(): lax.psum_scatter(part_out.astype(jnp.bfloat16), 'dp', scatter_dimension=2...]
    all_gather x1, waiting for transfers between devices: 0.02 us -> 32.7 us  [shards(): lax.all_gather(v_out, 'dp', axis=2, tiled=True)]
    all_to_all x1, waiting for transfers between devices: 0.01 us -> 15.2 us  [shards(): lax.all_to_all(send_u, ('tensor', 'expert'), split_axis=0, concat_axis=0,...]
    all_to_all x1, waiting for transfers between devices: 14.6 us -> 0.01 us  [shards(): lax.all_to_all(send_dy, ('tensor', 'expert'), split_axis=0, concat_axis=0...]
    all_gather x1, waiting for transfers between devices: 32.3 us -> 43 us  [shards(): lax.all_gather(w_out, 'dp', axis=2, tiled=True)]
  transfers between devices with their start and end apart: 11 -> 11, of which waited for: 9 -> 9; matrix products, arithmetic and copies ran while one was open for 13% -> 20% of each run, Pallas kernels for 0% -> 0%
where the time goes in v1:
time: 489 us; the launch traced here: 488 us
  waiting for transfers between devices  345 us (71%)
  matrix products  42 us (9%)
  other arithmetic  32.5 us (7%)
  starting transfers between devices  27.2 us (6%)
  local copies, waits for them, and re-layouts  26.5 us (5%)
  between operations  14.5 us (3%)
    all_gather x1, waiting for transfers between devices, shards(): lax.all_gather(v_in, 'dp', axis=3, tiled=True)  75.5 us
    reduce_scatter x1, waiting for transfers between devices, shards(): lax.psum_scatter(part_in.astype(jnp.bfloat16), 'dp', scatter_dimension=3,...  74.5 us
    all_gather x1, waiting for transfers between devices, shards(): lax.all_gather(own_sums.astype(jnp.bfloat16), 'tensor')  62.4 us
    all_gather x1, waiting for transfers between devices, shards(): lax.all_gather(w_out, 'dp', axis=2, tiled=True)  43 us
    all_gather x1, waiting for transfers between devices, shards(): lax.all_gather(v_out, 'dp', axis=2, tiled=True)  32.7 us
    all_to_all x1, waiting for transfers between devices, shards(): lax.all_to_all(partial_value, ('tensor', 'expert'), split_axis=0, concat_...  22.6 us
    all_to_all x1, waiting for transfers between devices, shards(): lax.all_to_all(send_u, ('tensor', 'expert'), split_axis=0, concat_axis=0,...  15.2 us
    all_to_all x1, waiting for transfers between devices, shards(): lax.all_to_all(send_x, ('tensor', 'expert'), split_axis=0, concat_axis=0,...  13.9 us
  transfers between devices with their start and end apart: 11, of which 9 were waited for; matrix products, arithmetic and copies ran while one was open for 20% of the time, Pallas kernels for 0%

profile of v1, /device:TPU:0, one launch (start us, length us, event | category | flops | bytes accessed | tf_op | source)
XLA Modules:
  0.0 487.9 jit_solution(8622860034079804569)
XLA Ops:
  9.7 4.5 reduce-window.6
  15.0 6.5 %scatter_custom_fusion.2 = bf16[192,2048]{1,0:T(8,128)(2,1)S(1)} fusion(s32[1024]{0:T(1024)S(1)} %bitcast.257, bf16[128,2048]{1,0:T(8,128)(2,1)S(1)} %copy-done, bf16[]{:T(256)} %constant.43.clone.1), kind=kCustom, calls=%fused_computation.23 | custom fusion | bytes 1310722 | tf_op jit(solution)/shard_map/scatter | solution.py:68
  22.7 7.5 %all-to-all-start.2 = ((bf16[16,1,12,2048]{3,2,1,0:T(8,128)(2,1)}), bf16[16,1,12,2048]{3,2,1,0:T(8,128)(2,1)S(1)}, u32[]{:S(2)}, u32[]{:S(2)}) async-start(bf16[16,1,12,2048]{3,2,1,0:T(8,128)(2,1)} %bitcast.30), calls=%async_computation.2 | async-start | bytes 2097152 | tf_op jit(solution)/shard_map/all_to_all | solution.py:72
  30.3 6.5 %scatter_custom_fusion.1 = bf16[192,2048]{1,0:T(8,128)(2,1)S(1)} fusion(s32[1024]{0:T(1024)S(1)} %bitcast.258, bf16[128,2048]{1,0:T(8,128)(2,1)S(1)} %copy-done.5, bf16[]{:T(256)} %constant.43.clone.1), kind=kCustom, calls=%fused_computation.25 | custom fusion | bytes 1310722 | tf_op jit(solution)/shard_map/scatter | solution.py:67
  37.9 15.2 %all-to-all-done.2 = bf16[16,1,12,2048]{3,2,1,0:T(8,128)(2,1)S(1)} async-done(((bf16[16,1,12,2048]{3,2,1,0:T(8,128)(2,1)}), bf16[16,1,12,2048]{3,2,1,0:T(8,128)(2,1)S(1)}, u32[]{:S(2)}, u32[]{:S(2)}) %all-to-all-start.2) | async-done | bytes 786464 | tf_op jit(solution)/shard_map/all_to_all | solution.py:72
  53.1 6.8 %all-to-all-start.1 = ((bf16[16,1,12,2048]{3,2,1,0:T(8,128)(2,1)}), bf16[16,1,12,2048]{3,2,1,0:T(8,128)(2,1)}, u32[]{:S(2)}, u32[]{:S(2)}) async-start(bf16[16,1,12,2048]{3,2,1,0:T(8,128)(2,1)} %bitcast.14), calls=%async_computation.1 | async-start | bytes 2097152 | tf_op jit(solution)/shard_map/all_to_all | solution.py:71
  60.9 6.9 %scatter_custom_fusion = bf16[192,2048]{1,0:T(8,128)(2,1)S(1)} fusion(s32[1024]{0:T(1024)S(1)} %bitcast.259, f32[128,2048]{1,0:T(8,128)S(1)} %convert_element_type.84, f32[1024]{0:T(1024)S(1)} %mul.184, bf16[]{:T(256)} %constant.43.clone.1), kind=kCustom, calls=%fused_computation.22 | custom fusion | flops 4194304 | bytes 1839106 | tf_op jit(solution)/shard_map/scatter | solution.py:69
  69.0 13.9 %all-to-all-done.1 = bf16[16,1,12,2048]{3,2,1,0:T(8,128)(2,1)} async-done(((bf16[16,1,12,2048]{3,2,1,0:T(8,128)(2,1)}), bf16[16,1,12,2048]{3,2,1,0:T(8,128)(2,1)}, u32[]{:S(2)}, u32[]{:S(2)}) %all-to-all-start.1) | async-done | bytes 786464 | tf_op jit(solution)/shard_map/all_to_all | solution.py:71
  82.9 6.8 %all-to-all-start = ((bf16[16,1,12,2048]{3,2,1,0:T(8,128)(2,1)}), bf16[16,1,12,2048]{3,2,1,0:T(8,128)(2,1)S(1)}, u32[]{:S(2)}, u32[]{:S(2)}) async-start(bf16[16,1,12,2048]{3,2,1,0:T(8,128)(2,1)} %bitcast.6), calls=%async_computation | async-start | bytes 2097152 | tf_op jit(solution)/shard_map/all_to_all | solution.py:73
  92.7 6.4 %fusion.44 = f32[16,1,12,2,768]{4,0,2,3,1:T(8,128)} fusion(bf16[1,2,768,2048]{3,2,1,0:T(8,128)(2,1)} %all-gather.9.cloned.1.call-done, bf16[16,1,12,2048]{3,2,1,0:T(8,128)(2,1)} %all-to-all-done.1), kind=kOutput, calls=%fused_computation.41 | convolution fusion | flops 1207959552 | bytes 8257536 | tf_op jit(solution)/shard_map/nesd,egfd->nesgf/dot_general | solution.py:9
  99.1 75.5 %all-gather.13.cloned.1.call-done = bf16[1,2,768,2048]{3,2,1,0:T(8,128)(2,1)} async-done(((bf16[1,2,768,1024]{3,2,1,0:T(8,128)(2,1)}), bf16[1,2,768,2048]{3,2,1,0:T(8,128)(2,1)}) %all-gather.13.cloned.1.call-update) | async-done | bytes 6291472 | tf_op jit(solution)/shard_map/all_gather | solution.py:48
  174.6 5.5 %fusion.6 = f32[16,12,2,768]{3,0,1,2:T(8,128)S(1)} fusion(bf16[1,2,768,2048]{3,2,1,0:T(8,128)(2,1)} %all-gather.13.cloned.1.call-done, bf16[16,1,12,2048]{3,2,1,0:T(8,128)(2,1)} %all-to-all-done.1), kind=kOutput, calls=%fused_computation.14 | convolution fusion | flops 1207959552 | bytes 8257536 | tf_op jit(solution)/shard_map/nesd,egfd->nesgf/dot_general | solution.py:11
  183.5 4.9 %fusion.26 = bf16[1,768,2048]{2,1,0:T(8,128)(2,1)} fusion(bf16[16,1,12,2048]{3,2,1,0:T(8,128)(2,1)S(1)} %all-to-all-done, f32[16,1,12,2,768]{4,0,2,3,1:T(8,128)} %fusion.50, f32[16,1,12,2,768]{4,0,2,3,1:T(8,128)} %fusion.44), kind=kOutput, calls=%fused_computation.33 | convolution fusion | flops 607469568 | bytes 6291456 | tf_op jit(solution)/shard_map/nesf,nesd->efd/dot_general | solution.py:33
  188.4 32.7 %all-gather.7.cloned.1.call-done = bf16[1,768,2048]{2,1,0:T(8,128)(2,1)} async-done(((bf16[1,768,1024]{2,1,0:T(8,128)(2,1)}), bf16[1,768,2048]{2,1,0:T(8,128)(2,1)}) %all-gather.7.cloned.1.call-update) | async-done | bytes 3145744 | tf_op jit(solution)/shard_map/all_gather | solution.py:50
  224.4 43.0 %all-gather.11.cloned.1.call-done = bf16[1,768,2048]{2,1,0:T(8,128)(2,1)} async-done(((bf16[1,768,1024]{2,1,0:T(8,128)(2,1)}), bf16[1,768,2048]{2,1,0:T(8,128)(2,1)}) %all-gather.11.cloned.1.call-update) | async-done | bytes 3145744 | tf_op jit(solution)/shard_map/all_gather | solution.py:49
  267.4 4.5 fusion.94
  279.8 5.6 %all-to-all-start.3 = ((bf16[16,1,12,2048]{3,2,1,0:T(8,128)(2,1)}), bf16[16,1,12,2048]{3,2,1,0:T(8,128)(2,1)S(1)}, u32[]{:S(2)}, u32[]{:S(2)}) async-start(bf16[16,1,12,2048]{3,2,1,0:T(8,128)(2,1)} %copy.63), calls=%async_computation.3 | async-start | bytes 2097152 | tf_op jit(solution)/shard_map/all_to_all | solution.py:78
  285.6 22.6 %all-to-all-done.3 = bf16[16,1,12,2048]{3,2,1,0:T(8,128)(2,1)S(1)} async-done(((bf16[16,1,12,2048]{3,2,1,0:T(8,128)(2,1)}), bf16[16,1,12,2048]{3,2,1,0:T(8,128)(2,1)S(1)}, u32[]{:S(2)}, u32[]{:S(2)}) %all-to-all-start.3) | async-done | bytes 786464 | tf_op jit(solution)/shard_map/all_to_all | solution.py:78
  308.4 6.9 %gather_fusion = f32[1024,2048]{1,0:T(8,128)} fusion(f32[192,2048]{1,0:T(8,128)S(1)} %reshape.400, s32[1024]{0:T(1024)S(1)} %broadcast_clamp_fusion), kind=kCustom, calls=%fused_computation | custom fusion | bytes 16781312 | tf_op jit(solution)/shard_map/gather | solution.py:82
  315.2 7.8 %fusion.1 = bf16[128,2048]{1,0:T(8,128)(2,1)} fusion(f32[1024,2048]{1,0:T(8,128)} %gather_fusion, pred[128,8]{1,0:T(8,128)(4,1)S(1)} %fusion.99), kind=kLoop, calls=%fused_computation.7 | loop fusion | flops 3932160 | bytes 8913920 | tf_op jit(solution)/shard_map/reduce_sum | solution.py:84
  325.1 6.0 %fusion.3 = bf16[1,2,768,2048]{3,2,1,0:T(8,128)(2,1)} fusion(f32[2,768,2048,1]{2,1,3,0:T(8,128)S(1)} %fusion.59, bf16[16,12,1,768]{3,0,1,2:T(8,128)(2,1)S(1)} %copy-done.12, bf16[16,12,1,768]{3,0,1,2:T(8,128)(2,1)S(1)} %copy-done.14, bf16[16,1,12,2048]{3,2,1,0:T(8,128)(2,1)} %all-to-all-done.1), kind=kOutput, calls=%fused_computation.10 | convolution fusion | flops 1214545920 | bytes 20250624 | tf_op jit(solution)/shard_map/nesd,nesgf->egfd/dot_general | solution.py:32
  334.7 62.4 %all-gather.15.cloned.1.call-done = bf16[1024,2048]{1,0:T(8,128)(2,1)} async-done(((bf16[128,2048]{1,0:T(8,128)(2,1)}), bf16[1024,2048]{1,0:T(8,128)(2,1)}) %all-gather.15.cloned.1.call-update) | async-done | bytes 4194320 | tf_op jit(solution)/shard_map/all_gather | solution.py:85
  401.2 74.5 %reduce-scatter.3.cloned.1.call-done = bf16[1,2,768,1024]{3,2,1,0:T(8,128)(2,1)} async-done(((bf16[1,2,768,2048]{3,2,1,0:T(8,128)(2,1)}), bf16[1,2,768,1024]{3,2,1,0:T(8,128)(2,1)}) %reduce-scatter.3.cloned.1.call-update) | async-done | bytes 3145744 | tf_op jit(solution)/shard_map/reduce_scatter | solution.py:89
  475.8 5.3 %convert_element_type.96 = f32[1,2,768,1024]{3,2,1,0:T(8,128)} convert(bf16[1,2,768,1024]{3,2,1,0:T(8,128)(2,1)} %reduce-scatter.3.cloned.1.call-done) | non-fusion elementwise | flops 1572864 | bytes 9437184 | tf_op jit(solution)/shard_map/convert_element_type | solution.py:91
  (90 shorter events, 34.9 us)
Async XLA Ops:
  7.2 7.8 %copy-start = (bf16[128,2048]{1,0:T(8,128)(2,1)S(1)}, bf16[128,2048]{1,0:T(8,128)(2,1)}, u32[]{:S(2)}) copy-start(bf16[128,2048]{1,0:T(8,128)(2,1)} %param.10) | copy-start | bytes 1572868
  7.2 85.5 %all-gather.9.cloned.1.call-start = ((), (), s32[]{:S(2)}) async-start(), calls=%async_computation.7 | async-start | bytes 9437184 | tf_op jit(solution)/shard_map/all_gather | solution.py:47
  7.9 166.7 %all-gather.13.cloned.1.call-start = ((), (), s32[]{:S(2)}) async-start(), calls=%async_computation.9 | async-start | bytes 9437184 | tf_op jit(solution)/shard_map/all_gather | solution.py:48
  8.7 21.6 %copy-start.5 = (bf16[128,2048]{1,0:T(8,128)(2,1)S(1)}, bf16[128,2048]{1,0:T(8,128)(2,1)}, u32[]{:S(2)}) copy-start(bf16[128,2048]{1,0:T(8,128)(2,1)} %param.9) | copy-start | bytes 1572868
  8.7 212.4 %all-gather.7.cloned.1.call-start = ((), (), s32[]{:S(2)}) async-start(), calls=%async_computation.6 | async-start | bytes 4718592 | tf_op jit(solution)/shard_map/all_gather | solution.py:50
  22.7 37.8 %copy-start.8 = (f32[128,8]{0,1:T(8,128)S(1)}, f32[128,8]{0,1:T(8,128)}, u32[]{:S(2)}) copy-start(f32[128,8]{0,1:T(8,128)} %param.13) | copy-start | bytes 12292
  22.7 38.1 %copy-start.6 = (bf16[128,2048]{1,0:T(8,128)(2,1)S(1)}, bf16[128,2048]{1,0:T(8,128)(2,1)}, u32[]{:S(2)}) copy-start(bf16[128,2048]{1,0:T(8,128)(2,1)} %param.11) | copy-start | bytes 1572868
  22.7 30.4 %all-to-all-start.2 = ((bf16[16,1,12,2048]{3,2,1,0:T(8,128)(2,1)}), bf16[16,1,12,2048]{3,2,1,0:T(8,128)(2,1)S(1)}, u32[]{:S(2)}, u32[]{:S(2)}) async-start(bf16[16,1,12,2048]{3,2,1,0:T(8,128)(2,1)} %bitcast.30), calls=%async_computation.2 | async-start | bytes 2097152 | tf_op jit(solution)/shard_map/all_to_all | solution.py:72
  53.1 127.0 %copy-start.3 = (bf16[16,1,12,2048]{3,2,1,0:T(8,128)(2,1)}, bf16[16,1,12,2048]{3,2,1,0:T(8,128)(2,1)S(1)}, u32[]{:S(2)}) copy-start(bf16[16,1,12,2048]{3,2,1,0:T(8,128)(2,1)S(1)} %all-to-all-done.2) | copy-start | bytes 2359300
  53.1 29.8 %all-to-all-start.1 = ((bf16[16,1,12,2048]{3,2,1,0:T(8,128)(2,1)}), bf16[16,1,12,2048]{3,2,1,0:T(8,128)(2,1)}, u32[]{:S(2)}, u32[]{:S(2)}) async-start(bf16[16,1,12,2048]{3,2,1,0:T(8,128)(2,1)} %bitcast.14), calls=%async_computation.1 | async-start | bytes 2097152 | tf_op jit(solution)/shard_map/all_to_all | solution.py:71
  60.0 207.4 %all-gather.11.cloned.1.call-start = ((), (), s32[]{:S(2)}) async-start(), calls=%async_computation.8 | async-start | bytes 4718592 | tf_op jit(solution)/shard_map/all_gather | solution.py:49
  82.9 100.5 %all-to-all-start = ((bf16[16,1,12,2048]{3,2,1,0:T(8,128)(2,1)}), bf16[16,1,12,2048]{3,2,1,0:T(8,128)(2,1)S(1)}, u32[]{:S(2)}, u32[]{:S(2)}) async-start(bf16[16,1,12,2048]{3,2,1,0:T(8,128)(2,1)} %bitcast.6), calls=%async_computation | async-start | bytes 2097152 | tf_op jit(solution)/shard_map/all_to_all | solution.py:73
  89.7 241.4 %reduce-scatter.5.cloned.1.call-start = ((), (), s32[]{:S(2)}) async-start(), calls=%async_computation.11 | async-start | bytes 4718592 | tf_op jit(solution)/shard_map/reduce_scatter | solution.py:92
  174.6 5.5 %copy-start.2 = (bf16[1,2,768,2048]{3,2,1,0:T(8,128)(2,1)S(1)}, bf16[1,2,768,2048]{3,2,1,0:T(8,128)(2,1)}, u32[]{:S(2)}) copy-start(bf16[1,2,768,2048]{3,2,1,0:T(8,128)(2,1)} %all-gather.9.cloned.1.call-done) | copy-start | bytes 18874372
  267.4 9.1 %slice-start = ((s8[6291456]{0:T(1024)(128)(4,1)}), s8[2097152]{0:T(1024)(128)(4,1)S(1)}, s32[]{:S(2)}) async-start(s8[6291456]{0:T(1024)(128)(4,1)} %bitcast.260), calls=%async_computation.13 | async-start | bytes 4194304
  272.0 4.6 copy-start.11
  272.0 4.6 copy-start.13
  272.0 4.7 slice-start.1
  279.8 28.4 %all-to-all-start.3 = ((bf16[16,1,12,2048]{3,2,1,0:T(8,128)(2,1)}), bf16[16,1,12,2048]{3,2,1,0:T(8,128)(2,1)S(1)}, u32[]{:S(2)}, u32[]{:S(2)}) async-start(bf16[16,1,12,2048]{3,2,1,0:T(8,128)(2,1)} %copy.63), calls=%async_computation.3 | async-start | bytes 2097152 | tf_op jit(solution)/shard_map/all_to_all | solution.py:78
  285.3 111.9 %all-gather.15.cloned.1.call-start = ((), (), s32[]{:S(2)}) async-start(), calls=%async_computation.12 | async-start | bytes 4718592 | tf_op jit(solution)/shard_map/all_gather | solution.py:85
  315.2 7.9 %copy-start.4 = (bf16[16,1,12,2048]{3,2,1,0:T(8,128)(2,1)S(1)}, bf16[16,1,12,2048]{3,2,1,0:T(8,128)(2,1)}, u32[]{:S(2)}) copy-start(bf16[16,1,12,2048]{3,2,1,0:T(8,128)(2,1)} %copy-done.3) | copy-start | bytes 2359300
  315.2 7.9 %copy-start.10 = (bf16[16,12,1,768]{3,0,1,2:T(8,128)(2,1)S(1)}, bf16[16,12,1,768]{3,0,1,2:T(8,128)(2,1)}, u32[]{:S(2)}) copy-start(bf16[16,12,1,768]{3,0,1,2:T(8,128)(2,1)} %copy-done.9) | copy-start | bytes 884740
  323.0 152.7 %reduce-scatter.3.cloned.1.call-start = ((), (), s32[]{:S(2)}) async-start(), calls=%async_computation.10 | async-start | bytes 9437184 | tf_op jit(solution)/shard_map/reduce_scatter | solution.py:89
  400.1 81.0 %copy-start.1 = (bf16[128,2048]{1,0:T(8,128)(2,1)S(1)}, bf16[128,2048]{1,0:T(8,128)(2,1)}, u32[]{:S(2)}) copy-start(bf16[128,2048]{1,0:T(8,128)(2,1)} %param.10) | copy-start | bytes 1572868
  (4 other events, 10.9 us)
Sparse Core Ops, SparseCore 0:
  9.5 83.0 all-gather.8
  94.2 80.3 all-gather.12
  176.1 44.8 all-gather.6
  222.5 44.8 all-gather.10
  270.1 43.4 reduce-scatter.4
  323.1 73.9 all-gather.14
  400.0 75.6 reduce-scatter.2
